TPU v7x, 32 devices: a whole 2x2x4 slice. The times are simulated.
32 devices in a mesh: gx: 2 (over y), gz: 4 (over x, core), ga: 4 (over z).
Axes of the slice: x: 2, y: 2, z: 4, core: 2. Of those that a mesh axis runs over, the one named last changes fastest.
Arguments:
- right_side: float32 [32, 128, 512], P('gx', 'ga', 'gz'), may hold values from -60 to 60, as said below
- diagonal: float32 [32, 128, 512], P('gx', 'ga', 'gz'), may hold values from 0.02 to 1
- element_features: bfloat16 [256, 4096], P(None, ('gx', 'gz', 'ga')), may hold values from -6 to 6
- sample_bank: bfloat16 [256, 131072], P(None, ('gx', 'gz', 'ga')), may hold values from -6 to 6
- target_bank: bfloat16 [6, 131072], P(None, ('gx', 'gz', 'ga')), may hold values from -6 to 6
- patch_index: int32 [65536], P(('gx', 'gz', 'ga')), may hold values from 0 to 4095
- w_first: bfloat16 [256, 256], replicated, may hold values from -0.375 to 0.375
- w_second: bfloat16 [256, 256], replicated, may hold values from -0.375 to 0.375
- w_third: bfloat16 [6, 256], replicated, may hold values from -0.375 to 0.375
Outputs:
- pressure: float32 [32, 128, 512], P('gx', 'ga', 'gz')
- residual: float32 [32, 128, 512], P('gx', 'ga', 'gz')
- step_first: float32 [256, 256], replicated
- step_second: float32 [256, 256], replicated
- step_third: float32 [6, 256], replicated
Inputs may be any that keep to these rules, and one draw needn't show every extreme that they name: `right_side`: grows in magnitude along the first dimension. `patch_index`: each entry names a column of the sample_bank and target_bank block that lies on the same device as the entry.
All inputs are finite; a program needn't handle non-finite values.
Results may differ from a plain program's by a relative error of at most 0.0004.
The roundings to bfloat16 on the way count: a program that leaves them out, or rounds other values in their place, can miss the bound.
Values sent between devices are 32-bit elements; how exact they have to be, the bound alone decides.
A program may use at most 64 MiB of HBM per device.

v0:
```python
import jax
import jax.numpy as jnp
from jax import lax
from jax.sharding import PartitionSpec as P

EL = 8
ITERS = 12


taps = (1.6, -0.2, 8.0 / 315.0, -1.0 / 560.0)
center = 3.0 * 205.0 / 72.0
epsilon = 1e-06


def with_halo(array, sides, width):
    for axis, dim in sides:
        count, length = (lax.axis_size(axis), array.shape[dim])
        up = [(i, (i + 1) % count) for i in range(count - 1)]
        down = [(j, i) for i, j in up]
        last = lax.slice_in_dim(array, length - width, length, axis=dim)
        initial = lax.slice_in_dim(array, 0, width, axis=dim)
        before = lax.ppermute(last, axis, up)
        after = lax.ppermute(initial, axis, down)
        array = jnp.concatenate([before, array, after], axis=dim)
    return array


def neighbours(padded):
    length_x = padded.shape[0] - 8
    length_y = padded.shape[1] - 8
    length_z = padded.shape[2] - 8
    summed = jnp.zeros((length_x, length_y, length_z), padded.dtype)
    for offset in range(1, 5):
        weight = taps[offset - 1]
        along_x = (
            padded[4 + offset : 4 + offset + length_x, 4 : 4 + length_y, 4 : 4 + length_z]
            + padded[4 - offset : 4 - offset + length_x, 4 : 4 + length_y, 4 : 4 + length_z]
        )
        along_y = (
            padded[4 : 4 + length_x, 4 + offset : 4 + offset + length_y, 4 : 4 + length_z]
            + padded[4 : 4 + length_x, 4 - offset : 4 - offset + length_y, 4 : 4 + length_z]
        )
        along_z = (
            padded[4 : 4 + length_x, 4 : 4 + length_y, 4 + offset : 4 + offset + length_z]
            + padded[4 : 4 + length_x, 4 : 4 + length_y, 4 - offset : 4 - offset + length_z]
        )
        summed = summed + weight * (along_x + along_y + along_z)
    return summed


def apply_operator(field, precond):
    padded = with_halo(field, (("gx", 0), ("ga", 1), ("gz", 2)), 4)
    return precond * field - neighbours(padded)


def paired_sums(residual, scaled, image_dir):
    return lax.psum((jnp.sum(residual * scaled), jnp.sum(scaled * image_dir)), ("gx", "gz", "ga"))


def closure(w_first, w_second, w_third, inputs):
    linear_first = jnp.dot(w_first, inputs, preferred_element_type=jnp.float32)
    hidden_first = jax.nn.silu(linear_first).astype(jnp.bfloat16)
    linear_second = jnp.dot(w_second, hidden_first, preferred_element_type=jnp.float32)
    hidden_second = jax.nn.silu(linear_second).astype(jnp.bfloat16)
    predicted = jnp.dot(w_third, hidden_second, preferred_element_type=jnp.float32)
    return (linear_first, hidden_first, linear_second, hidden_second, predicted)


def slope(linear):
    sigmoid = jax.nn.sigmoid(linear)
    return sigmoid * (1.0 + linear * (1.0 - sigmoid))


def gradients(w_first, w_second, w_third, inputs, targets):
    linear_first, hidden_first, linear_second, hidden_second, predicted = closure(
        w_first, w_second, w_third, inputs
    )
    error = (predicted - targets.astype(jnp.float32)).astype(jnp.bfloat16)
    contract = (((1,), (1,)), ((), ()))
    leading = (((0,), (0,)), ((), ()))
    grad_third = lax.dot_general(error, hidden_second, contract, preferred_element_type=jnp.float32)
    back_second = lax.dot_general(w_third, error, leading, preferred_element_type=jnp.float32)
    delta_second = (back_second * slope(linear_second)).astype(jnp.bfloat16)
    grad_second = lax.dot_general(
        delta_second, hidden_first, contract, preferred_element_type=jnp.float32
    )
    back_first = lax.dot_general(
        w_second, delta_second, leading, preferred_element_type=jnp.float32
    )
    delta_first = (back_first * slope(linear_first)).astype(jnp.bfloat16)
    grad_first = lax.dot_general(delta_first, inputs, contract, preferred_element_type=jnp.float32)
    return (grad_first, grad_second, grad_third)


def normalize(gradient):
    return gradient * lax.rsqrt(jnp.mean(gradient * gradient) + epsilon)


def body(
    right_side,
    diagonal,
    element_features,
    sample_bank,
    target_bank,
    patch_index,
    w_first,
    w_second,
    w_third,
):
    predicted = closure(w_first, w_second, w_third, element_features)[4]
    trace = (predicted[0] + predicted[1] + predicted[2]) / 3.0
    length_x, length_y, length_z = right_side.shape
    blocks = trace.reshape(length_x // EL, length_y // EL, length_z // EL)
    forcing = jnp.broadcast_to(
        blocks[:, None, :, None, :, None],
        (length_x // EL, EL, length_y // EL, EL, length_z // EL, EL),
    )
    source = right_side + forcing.reshape(length_x, length_y, length_z)
    precond = diagonal + center
    pressure = jnp.zeros_like(source)
    residual = source
    scaled = residual / precond
    image_dir = apply_operator(scaled, precond)
    product_now, curvature = paired_sums(residual, scaled, image_dir)
    step_len = product_now / curvature
    direction = scaled
    along = image_dir
    for iteration in range(ITERS):
        pressure = pressure + step_len * direction
        residual = residual - step_len * along
        if iteration + 1 < ITERS:
            scaled = residual / precond
            image_dir = apply_operator(scaled, precond)
            product_next, curvature = paired_sums(residual, scaled, image_dir)
            ratio_next = product_next / product_now
            step_len = product_next / (curvature - ratio_next * product_next / step_len)
            direction = scaled + ratio_next * direction
            along = image_dir + ratio_next * along
            product_now = product_next
    inputs = jnp.take(sample_bank, patch_index, axis=1)
    targets = jnp.take(target_bank, patch_index, axis=1)
    grad_first, grad_second, grad_third = gradients(w_first, w_second, w_third, inputs, targets)
    grad_first, grad_second, grad_third = lax.psum(
        (grad_first, grad_second, grad_third), ("gx", "gz", "ga")
    )
    step_first = normalize(grad_first)
    step_second = normalize(grad_second)
    step_third = normalize(grad_third)
    return (pressure, residual, step_first, step_second, step_third)


def solution(mesh):
    return jax.shard_map(
        body,
        mesh=mesh,
        in_specs=(
            P("gx", "ga", "gz"),
            P("gx", "ga", "gz"),
            P(None, ("gx", "gz", "ga")),
            P(None, ("gx", "gz", "ga")),
            P(None, ("gx", "gz", "ga")),
            P(("gx", "gz", "ga")),
            P(),
            P(),
            P(),
        ),
        out_specs=(P("gx", "ga", "gz"), P("gx", "ga", "gz"), P(), P(), P()),
        check_vma=False,
    )
```

profile of v0, /device:TPU:0, one launch (start us, length us, event | category | flops | bytes accessed | tf_op | source)
XLA Modules:
  0.0 1036.6 jit_solution(6138457786089235416)
XLA Ops:
  12.0 3.7 reshape.37
  15.8 4.9 collective-permute-start.1
  22.6 4.3 collective-permute-done
  26.9 3.5 collective-permute-start.3
  32.1 4.3 collective-permute-done.2
  44.1 45.5 %all-reduce.11 = (f32[]{:T(128)}, f32[]{:T(128)}) all-reduce(f32[]{:T(128)} %get-tuple-element.28, f32[]{:T(128)} %get-tuple-element.27), channel_id=1, replica_groups=mesh['gx'=2,'gz'=4,'ga'=4] {'gx','gz','ga'}, use_global_device_ids=true, to_apply=%region_1.2 | all-reduce | flops 2 | bytes 16 | tf_op jit(solution)/shard_map/psum | solution.py:57
  91.1 4.4 collective-permute-start.7
  97.4 4.3 collective-permute-done.6
  105.5 4.3 collective-permute-done.8
  117.5 46.0 %all-reduce.10 = (f32[]{:T(128)}, f32[]{:T(128)}) all-reduce(f32[]{:T(128)} %get-tuple-element.26, f32[]{:T(128)} %get-tuple-element.25), channel_id=1, replica_groups=mesh['gx'=2,'gz'=4,'ga'=4] {'gx','gz','ga'}, use_global_device_ids=true, to_apply=%region_5.6 | all-reduce | flops 2 | bytes 16 | tf_op jit(solution)/shard_map/psum | solution.py:57
  168.3 4.4 collective-permute-start.13
  174.6 4.3 collective-permute-done.12
  182.7 4.3 collective-permute-done.14
  194.7 46.0 %all-reduce.9 = (f32[]{:T(128)}, f32[]{:T(128)}) all-reduce(f32[]{:T(128)} %get-tuple-element.24, f32[]{:T(128)} %get-tuple-element.23), channel_id=1, replica_groups=mesh['gx'=2,'gz'=4,'ga'=4] {'gx','gz','ga'}, use_global_device_ids=true, to_apply=%region_9.10 | all-reduce | flops 2 | bytes 16 | tf_op jit(solution)/shard_map/psum | solution.py:57
  244.9 4.4 collective-permute-start.19
  251.2 4.3 collective-permute-done.18
  259.3 4.3 collective-permute-done.20
  271.3 46.0 %all-reduce.8 = (f32[]{:T(128)}, f32[]{:T(128)}) all-reduce(f32[]{:T(128)} %get-tuple-element.22, f32[]{:T(128)} %get-tuple-element.21), channel_id=1, replica_groups=mesh['gx'=2,'gz'=4,'ga'=4] {'gx','gz','ga'}, use_global_device_ids=true, to_apply=%region_13.14 | all-reduce | flops 2 | bytes 16 | tf_op jit(solution)/shard_map/psum | solution.py:57
  321.4 4.4 collective-permute-start.25
  327.7 4.3 collective-permute-done.24
  335.8 4.3 collective-permute-done.26
  347.9 46.0 %all-reduce.7 = (f32[]{:T(128)}, f32[]{:T(128)}) all-reduce(f32[]{:T(128)} %get-tuple-element.20, f32[]{:T(128)} %get-tuple-element.19), channel_id=1, replica_groups=mesh['gx'=2,'gz'=4,'ga'=4] {'gx','gz','ga'}, use_global_device_ids=true, to_apply=%region_17.18 | all-reduce | flops 2 | bytes 16 | tf_op jit(solution)/shard_map/psum | solution.py:57
  398.1 4.4 collective-permute-start.31
  404.3 4.3 collective-permute-done.30
  412.5 4.3 collective-permute-done.32
  424.5 46.0 %all-reduce.6 = (f32[]{:T(128)}, f32[]{:T(128)}) all-reduce(f32[]{:T(128)} %get-tuple-element.18, f32[]{:T(128)} %get-tuple-element.17), channel_id=1, replica_groups=mesh['gx'=2,'gz'=4,'ga'=4] {'gx','gz','ga'}, use_global_device_ids=true, to_apply=%region_21.22 | all-reduce | flops 2 | bytes 16 | tf_op jit(solution)/shard_map/psum | solution.py:57
  475.2 4.4 collective-permute-start.37
  481.5 4.3 collective-permute-done.36
  493.8 9.0 gather_fusion
  512.7 47.0 %all-reduce.5 = (f32[]{:T(128)}, f32[]{:T(128)}) all-reduce(f32[]{:T(128)} %get-tuple-element.16, f32[]{:T(128)} %get-tuple-element.15), channel_id=1, replica_groups=mesh['gx'=2,'gz'=4,'ga'=4] {'gx','gz','ga'}, use_global_device_ids=true, to_apply=%region_25.26 | all-reduce | flops 2 | bytes 16 | tf_op jit(solution)/shard_map/psum | solution.py:57
  564.4 4.4 collective-permute-start.43
  575.6 3.5 collective-permute-start.45
  584.8 9.0 gather_fusion.1
  605.3 46.9 %all-reduce.4 = (f32[]{:T(128)}, f32[]{:T(128)}) all-reduce(f32[]{:T(128)} %get-tuple-element.14, f32[]{:T(128)} %get-tuple-element.13), channel_id=1, replica_groups=mesh['gx'=2,'gz'=4,'ga'=4] {'gx','gz','ga'}, use_global_device_ids=true, to_apply=%region_29.30 | all-reduce | flops 2 | bytes 16 | tf_op jit(solution)/shard_map/psum | solution.py:57
  657.5 4.4 collective-permute-start.49
  664.3 3.7 collective-permute-done.48
  683.7 46.2 %all-reduce.3 = (f32[]{:T(128)}, f32[]{:T(128)}) all-reduce(f32[]{:T(128)} %get-tuple-element.12, f32[]{:T(128)} %get-tuple-element.11), channel_id=1, replica_groups=mesh['gx'=2,'gz'=4,'ga'=4] {'gx','gz','ga'}, use_global_device_ids=true, to_apply=%region_33.34 | all-reduce | flops 2 | bytes 16 | tf_op jit(solution)/shard_map/psum | solution.py:57
  735.8 4.4 collective-permute-start.55
  741.5 4.1 fusion.5
  755.8 3.3 collective-permute-start.59
  762.7 48.6 %all-reduce.2 = (f32[]{:T(128)}, f32[]{:T(128)}) all-reduce(f32[]{:T(128)} %get-tuple-element.10, f32[]{:T(128)} %get-tuple-element.9), channel_id=1, replica_groups=mesh['gx'=2,'gz'=4,'ga'=4] {'gx','gz','ga'}, use_global_device_ids=true, to_apply=%region_37.38 | all-reduce | flops 2 | bytes 16 | tf_op jit(solution)/shard_map/psum | solution.py:57
  816.4 4.4 collective-permute-start.61
  823.6 3.4 collective-permute-done.60
  831.6 53.6 %all-reduce.15.cloned.1.call-done = (f32[256,256]{1,0:T(8,128)}, f32[256,256]{1,0:T(8,128)}) async-done(((f32[256,256]{1,0:T(8,128)}, f32[256,256]{1,0:T(8,128)}), (f32[256,256]{1,0:T(8,128)}, f32[256,256]{1,0:T(8,128)})) %all-reduce.15.cloned.1.call-update) | async-done | bytes 524304 | tf_op jit(solution)/shard_map/psum | solution.py:143
  896.1 45.7 %all-reduce.1 = (f32[]{:T(128)}, f32[]{:T(128)}) all-reduce(f32[]{:T(128)} %get-tuple-element.8, f32[]{:T(128)} %get-tuple-element.7), channel_id=1, replica_groups=mesh['gx'=2,'gz'=4,'ga'=4] {'gx','gz','ga'}, use_global_device_ids=true, to_apply=%region_41.42 | all-reduce | flops 2 | bytes 16 | tf_op jit(solution)/shard_map/psum | solution.py:57
  947.5 4.4 collective-permute-start.67
  958.1 3.3 collective-permute-start.69
  977.2 44.3 %all-reduce = (f32[]{:T(128)}, f32[]{:T(128)}, f32[6,256]{1,0:T(8,128)S(1)}) all-reduce(f32[]{:T(128)} %get-tuple-element.6, f32[]{:T(128)} %get-tuple-element.5, f32[6,256]{1,0:T(8,128)S(1)} %fusion.377), channel_id=1, replica_groups=mesh['gx'=2,'gz'=4,'ga'=4] {'gx','gz','ga'}, use_global_device_ids=true, to_apply=%region_45.46 | all-reduce | flops 1538 | bytes 12304 | tf_op jit(solution)/shard_map/psum | solution.py:57
  (322 shorter events, 210.1 us)
Async XLA Ops:
  7.2 878.1 %all-reduce.15.cloned.1.call-start = ((), (), s32[]{:S(2)}) async-start(), calls=%async_computation | async-start | bytes 1048576 | tf_op jit(solution)/shard_map/psum | solution.py:143
  15.8 6.8 collective-permute-start.1
  20.7 6.2 collective-permute-start
  26.9 5.2 collective-permute-start.3
  30.4 6.0 collective-permute-start.2
  91.1 6.3 collective-permute-start.7
  95.5 6.2 collective-permute-start.6
  103.8 6.0 collective-permute-start.8
  168.3 6.3 collective-permute-start.13
  172.7 6.2 collective-permute-start.12
  181.0 6.0 collective-permute-start.14
  244.9 6.3 collective-permute-start.19
  249.3 6.2 collective-permute-start.18
  257.6 6.0 collective-permute-start.20
  321.4 6.3 collective-permute-start.25
  325.8 6.2 collective-permute-start.24
  334.1 6.0 collective-permute-start.26
  398.1 6.3 collective-permute-start.31
  402.4 6.2 collective-permute-start.30
  410.7 6.0 collective-permute-start.32
  475.2 6.3 collective-permute-start.37
  479.6 6.2 collective-permute-start.36
  486.4 16.3 %collective-permute-start.39 = (f32[24,4,128]{2,1,0:T(4,128)}, f32[24,4,128]{2,1,0:T(4,128)}, u32[]{:S(2)}, u32[]{:S(2)}) collective-permute-start(f32[24,4,128]{2,1,0:T(4,128)} %get-tuple-element.166), channel_id=1, source_target_pairs={{0,1},{1,2},{2,3},{4,5},{5,6},{6,7},{8,9},{9,10},{10,11},{12,13},{... | collective-permute-start | bytes 147464 | tf_op jit(solution)/shard_map/ppermute | solution.py:22
  489.1 13.6 %collective-permute-start.38 = (f32[24,4,128]{2,1,0:T(4,128)}, f32[24,4,128]{2,1,0:T(4,128)}, u32[]{:S(2)}, u32[]{:S(2)}) collective-permute-start(f32[24,4,128]{2,1,0:T(4,128)} %get-tuple-element.167), channel_id=1, source_target_pairs={{1,0},{2,1},{3,2},{5,4},{6,5},{7,6},{9,8},{10,9},{11,10},{13,12},{... | collective-permute-start | bytes 147464 | tf_op jit(solution)/shard_map/ppermute | solution.py:23
  504.1 5.4 collective-permute-start.40
  505.4 4.6 collective-permute-start.41
  564.4 7.9 collective-permute-start.43
  568.8 6.2 collective-permute-start.42
  575.6 20.1 %collective-permute-start.45 = (f32[24,4,128]{2,1,0:T(4,128)}, f32[24,4,128]{2,1,0:T(4,128)S(1)}, u32[]{:S(2)}, u32[]{:S(2)}) collective-permute-start(f32[24,4,128]{2,1,0:T(4,128)} %get-tuple-element.162), channel_id=1, source_target_pairs={{0,1},{1,2},{2,3},{4,5},{5,6},{6,7},{8,9},{9,10},{10,11},{12,13},{... | collective-permute-start | bytes 147464 | tf_op jit(solution)/shard_map/ppermute | solution.py:22
  579.1 16.5 %collective-permute-start.44 = (f32[24,4,128]{2,1,0:T(4,128)}, f32[24,4,128]{2,1,0:T(4,128)S(1)}, u32[]{:S(2)}, u32[]{:S(2)}) collective-permute-start(f32[24,4,128]{2,1,0:T(4,128)} %get-tuple-element.163), channel_id=1, source_target_pairs={{1,0},{2,1},{3,2},{5,4},{6,5},{7,6},{9,8},{10,9},{11,10},{13,12},{... | collective-permute-start | bytes 147464 | tf_op jit(solution)/shard_map/ppermute | solution.py:23
  596.0 5.6 collective-permute-start.46
  657.5 6.8 collective-permute-start.49
  661.8 6.2 collective-permute-start.48
  668.0 5.1 collective-permute-start.51
  669.9 6.0 collective-permute-start.50
  735.8 9.8 collective-permute-start.55
  740.2 6.2 collective-permute-start.54
  746.4 5.9 collective-permute-start.57
  748.3 6.0 collective-permute-start.56
  754.5 4.7 collective-permute-start.58
  816.4 7.2 collective-permute-start.61
  820.8 6.2 collective-permute-start.60
  827.7 60.0 %collective-permute-start.63 = (f32[24,4,128]{2,1,0:T(4,128)}, f32[24,4,128]{2,1,0:T(4,128)S(1)}, u32[]{:S(2)}, u32[]{:S(2)}) collective-permute-start(f32[24,4,128]{2,1,0:T(4,128)} %get-tuple-element.150), channel_id=1, source_target_pairs={{0,1},{1,2},{2,3},{4,5},{5,6},{6,7},{8,9},{9,10},{10,11},{12,13},{... | collective-permute-start | bytes 147464 | tf_op jit(solution)/shard_map/ppermute | solution.py:22
  830.3 57.3 %collective-permute-start.62 = (f32[24,4,128]{2,1,0:T(4,128)}, f32[24,4,128]{2,1,0:T(4,128)S(1)}, u32[]{:S(2)}, u32[]{:S(2)}) collective-permute-start(f32[24,4,128]{2,1,0:T(4,128)} %get-tuple-element.151), channel_id=1, source_target_pairs={{1,0},{2,1},{3,2},{5,4},{6,5},{7,6},{9,8},{10,9},{11,10},{13,12},{... | collective-permute-start | bytes 147464 | tf_op jit(solution)/shard_map/ppermute | solution.py:23
  947.5 8.1 collective-permute-start.67
  951.9 6.2 collective-permute-start.66
  958.1 6.3 collective-permute-start.69
  961.4 6.0 collective-permute-start.68
  (69 other events, 1286.5 us)
Sparse Core Ops, SparseCore 0:
  752.4 132.7 all-reduce.14
where the time goes:
time: 1050 us; the launch traced here: 1040 us
  blocking collectives  554 us (53%)
  starting transfers between devices  167 us (16%)
  waiting for transfers between devices  150 us (14%)
  between operations  63.5 us (6%)
  other arithmetic  49.2 us (5%)
  local copies, waits for them, and re-layouts  34.4 us (3%)
  matrix products  17.4 us (2%)
    psum x12, blocking collectives, paired_sums(): lax.psum((jnp.sum(residual * scaled), jnp.sum(scaled * image_dir)), ('gx'...  554 us
    ppermute x36, starting transfers between devices, with_halo(): before = lax.ppermute(last, axis, up)  121 us
    ppermute x36, waiting for transfers between devices, with_halo(): after = lax.ppermute(initial, axis, down)  76.2 us
    psum x1, waiting for transfers between devices, body(): lax.psum((grad_first, grad_second, grad_third), ('gx', 'gz', 'ga'))  53.6 us
    ppermute x36, starting transfers between devices, with_halo(): after = lax.ppermute(initial, axis, down)  46.7 us
  transfers between devices with their start and end apart: 73, of which 47 were waited for; matrix products, arithmetic and copies ran while one was open for 5% of the time, Pallas kernels for 0%

commit v1 on v0

v1 whole, which is shorter than its diff:
```python
import functools

import jax
import jax.numpy as jnp
from jax import lax
from jax.experimental import pallas as pl
from jax.experimental.pallas import tpu as pltpu
from jax.sharding import PartitionSpec as P

EL = 8
ITERS = 12
TILE = 512
PHASES = (("gx", "gz"), ("ga",))
AXES = ("gx", "gz", "ga")

taps = (1.6, -0.2, 8.0 / 315.0, -1.0 / 560.0)
center = 3.0 * 205.0 / 72.0
epsilon = 1e-06
MESH = pl.DeviceIdType.MESH
F32 = jnp.float32
BF16 = jnp.bfloat16


def dot(a, b, dims=((1,), (0,)), precision=None):
    return lax.dot_general(a, b, (dims, ((), ())), preferred_element_type=F32, precision=precision)


def sigmoid(v):
    return 1.0 / (1.0 + jnp.exp(-v))


def grad_kernel(bank, target, index, w1, w2, w3, g1, g2, g3, counts):
    step = pl.program_id(0)
    rows = TILE // 128

    @pl.when(step == 0)
    def _():
        samples = index.shape[1]
        groups = counts.shape[0]
        ids = index[...]
        high = lax.broadcasted_iota(jnp.int32, (groups, samples), 0) == (ids // 128)
        low = lax.broadcasted_iota(jnp.int32, (128, samples), 0) == (ids % 128)
        counts[...] = dot(
            jnp.where(high, 1.0, 0.0).astype(BF16),
            jnp.where(low, 1.0, 0.0).astype(BF16),
            ((1,), (1,)),
        )
        g1[...] = jnp.zeros_like(g1)
        g2[...] = jnp.zeros_like(g2)
        g3[...] = jnp.zeros_like(g3)

    weight = jnp.concatenate([counts[pl.ds(step * rows + j, 1), :] for j in range(rows)], axis=1)
    x = bank[...]
    a1, a2, a3 = w1[...], w2[...], w3[...]
    l1 = dot(a1, x)
    s1 = sigmoid(l1)
    h1 = (l1 * s1).astype(BF16)
    l2 = dot(a2, h1)
    s2 = sigmoid(l2)
    h2 = (l2 * s2).astype(BF16)
    error = (dot(a3, h2) - target[...].astype(F32)).astype(BF16)

    def weighted(delta, right):
        scaled = delta.astype(F32) * weight
        upper = scaled.astype(BF16)
        lower = (scaled - upper.astype(F32)).astype(BF16)
        return dot(upper, right, ((1,), (1,))) + dot(lower, right, ((1,), (1,)))

    g3[...] += weighted(error, h2)
    d2 = (dot(a3, error, ((0,), (0,))) * (s2 * (1.0 + l2 * (1.0 - s2)))).astype(BF16)
    g2[...] += weighted(d2, h1)
    d1 = (dot(a2, d2, ((0,), (0,))) * (s1 * (1.0 + l1 * (1.0 - s1)))).astype(BF16)
    g1[...] += weighted(d1, x)


def closure_gradients(bank, target, index, w1, w2, w3):
    ch, columns = bank.shape
    stress = target.shape[0]
    whole = pl.BlockSpec(memory_space=pltpu.VMEM)
    fixed = lambda shape: pl.BlockSpec(shape, lambda i: (0, 0))
    return pl.pallas_call(
        grad_kernel,
        grid=(columns // TILE,),
        in_specs=[
            pl.BlockSpec((ch, TILE), lambda i: (0, i)),
            pl.BlockSpec((stress, TILE), lambda i: (0, i)),
            whole,
            whole,
            whole,
            whole,
        ],
        out_specs=[fixed((ch, ch)), fixed((ch, ch)), fixed((stress, ch))],
        out_shape=[
            jax.ShapeDtypeStruct((ch, ch), F32),
            jax.ShapeDtypeStruct((ch, ch), F32),
            jax.ShapeDtypeStruct((stress, ch), F32),
        ],
        scratch_shapes=[pltpu.VMEM((columns // 128, 128), F32)],
        compiler_params=pltpu.CompilerParams(dimension_semantics=("arbitrary",)),
        cost_estimate=pl.CostEstimate(
            flops=14 * ch * ch * columns, bytes_accessed=2 * ch * columns, transcendentals=4 * ch * columns
        ),
    )(bank, target, index.reshape(1, -1), w1, w2, w3)


def shift_offsets(sizes):
    combos = [()]
    for n in sizes:
        combos = [c + (k,) for c in combos for k in range(n)]
    return combos[1:]


def solve_kernel(
    sizes, right, diag, feats, w1, w2, w3, press, resid,
    mp, nb, wv, zv, sv, pv, inv, yp, yr, zp, zr, ar_src, ar_dst,
    h_send, h_recv, a_send, a_recv,
):
    lx, ly, lz = right.shape
    pos = {a: lax.axis_index(a) for a in AXES}

    def coords(axes, offs, sign):
        out = {}
        for a, k in zip(axes, offs):
            n = sizes[a]
            c = pos[a] + (k if sign > 0 else n - k) if k else pos[a]
            out[a] = lax.rem(c, n) if k else c
        return out

    def flat(axes, at):
        value = 0
        for a in axes:
            value = value * sizes[a] + at[a]
        return value

    groups = []
    for axes in PHASES:
        me = flat(axes, pos)
        peers = []
        for offs in shift_offsets([sizes[a] for a in axes]):
            to = {**pos, **coords(axes, offs, 1)}
            source = flat(axes, coords(axes, offs, -1))
            peers.append((to, source))
        groups.append((me, peers))

    mp[...] = jnp.zeros_like(mp)
    yr[...] = jnp.zeros_like(yr)
    zr[...] = jnp.zeros_like(zr)

    barrier = pltpu.get_barrier_semaphore()
    total = 0
    for _, peers in groups:
        for to, _ in peers:
            pl.semaphore_signal(barrier, inc=1, device_id=to, device_id_type=MESH)
            total += 1
    pl.semaphore_wait(barrier, total)

    lane = lax.broadcasted_iota(jnp.int32, (ly, lz), 1)
    sub8 = lax.broadcasted_iota(jnp.int32, (8, lz), 0)
    row_lane = lax.broadcasted_iota(jnp.int32, (1, lz), 1)

    def halo_copies(par):
        out = []

        def add(axis, step, number, src, dst):
            copy = pltpu.make_async_remote_copy(
                src_ref=src,
                dst_ref=dst,
                send_sem=h_send.at[number],
                recv_sem=h_recv.at[par, number],
                device_id={**pos, axis: jnp.clip(pos[axis] + step, 0, sizes[axis] - 1)},
                device_id_type=MESH,
            )
            can_send = pos[axis] < sizes[axis] - 1 if step > 0 else pos[axis] > 0
            will_get = pos[axis] > 0 if step > 0 else pos[axis] < sizes[axis] - 1
            out.append((copy, can_send, will_get))

        rows = pl.ds(8, ly)
        if sizes["gx"] > 1:
            add("gx", 1, 0, mp.at[par, pl.ds(lx, 4), rows], mp.at[par, pl.ds(0, 4), rows])
            add("gx", -1, 1, mp.at[par, pl.ds(4, 4), rows], mp.at[par, pl.ds(lx + 4, 4), rows])
        if sizes["ga"] > 1:
            add("ga", 1, 2, yp.at[par], yr.at[par, 0])
            add("ga", -1, 3, yp.at[par], yr.at[par, 1])
        if sizes["gz"] > 1:
            add("gz", 1, 4, zp.at[par], zr.at[par, 0])
            add("gz", -1, 5, zp.at[par], zr.at[par, 1])
        return out

    def halo_start(par):
        for copy, can_send, _ in halo_copies(par):
            pl.when(can_send)(copy.start)

    def halo_wait(par):
        for copy, _, will_get in halo_copies(par):
            pl.when(will_get)(copy.wait_recv)

    def halo_sent(par):
        for copy, can_send, _ in halo_copies(par):
            pl.when(can_send)(copy.wait_send)

    bases = []
    base = 0
    for axes in PHASES:
        bases.append(base)
        n = 1
        for a in axes:
            n *= sizes[a]
        base += n

    def sum_copies(par, phase):
        me, peers = groups[phase]
        out = []
        for k, (to, source) in enumerate(peers):
            slot = bases[phase]
            send = pltpu.make_async_remote_copy(
                src_ref=ar_src.at[par, phase],
                dst_ref=ar_dst.at[par, slot + me],
                send_sem=a_send.at[slot + k],
                recv_sem=a_recv.at[par, slot + me],
                device_id=to,
                device_id_type=MESH,
            )
            receive = pltpu.make_async_remote_copy(
                src_ref=ar_src.at[par, phase],
                dst_ref=ar_dst.at[par, slot + source],
                send_sem=a_send.at[slot + k],
                recv_sem=a_recv.at[par, slot + source],
                device_id=to,
                device_id_type=MESH,
            )
            out.append((send, receive))
        return out

    def sum_start(par, phase, row):
        ar_src[par, phase] = row
        ar_dst[par, bases[phase] + groups[phase][0]] = row
        for send, _ in sum_copies(par, phase):
            send.start()

    def sum_wait(par, phase):
        count = len(groups[phase][1]) + 1
        for _, receive in sum_copies(par, phase):
            receive.wait_recv()
        return jnp.sum(ar_dst[par, pl.ds(bases[phase], count)], axis=0)

    def sums_sent(par):
        for phase in range(len(PHASES)):
            for send, _ in sum_copies(par, phase):
                send.wait_send()

    def stencil_local(par):
        for x in range(lx):
            v = mp[par, 4 + x, pl.ds(8, ly)]
            acc = None
            for k in range(1, 5):
                t = mp[par, 4 + x, pl.ds(8 + k, ly)] + mp[par, 4 + x, pl.ds(8 - k, ly)]
                if x + k < lx:
                    t = t + mp[par, 4 + x + k, pl.ds(8, ly)]
                if x - k >= 0:
                    t = t + mp[par, 4 + x - k, pl.ds(8, ly)]
                t = t + jnp.where(lane >= k, pltpu.roll(v, k, 1), 0.0)
                t = t + jnp.where(lane < lz - k, pltpu.roll(v, lz - k, 1), 0.0)
                t = taps[k - 1] * t
                acc = t if acc is None else acc + t
            nb[x] = acc

    def z_correction(par):
        h = jnp.where(lane % 8 < 4, zr[par, 0], zr[par, 1])
        acc = jnp.zeros((ly, lz), F32)
        place = lane % 8
        for k in range(1, 5):
            ahead = jnp.where((place >= 4) & (place - 4 < k), pltpu.roll(h, k, 1), 0.0)
            behind = jnp.where((place < 4) & (place >= 4 - k), pltpu.roll(h, lz - k, 1), 0.0)
            acc = acc + taps[k - 1] * (ahead + behind)
        return acc

    def corrected(par, x, zc):
        acc = nb[x]
        for k in range(1, 5):
            if x - k < 0:
                acc = acc + taps[k - 1] * mp[par, 4 + x - k, pl.ds(8, ly)]
            if x + k >= lx:
                acc = acc + taps[k - 1] * mp[par, 4 + x + k, pl.ds(8, ly)]
        z = pltpu.roll(zc, (2 * lz - 8 * x - 4) % lz, 1)
        acc = acc + jnp.where((lane < 4) | (lane >= lz - 4), z, 0.0)
        h = jnp.where(sub8 < 4, yr[par, 1, x], yr[par, 0, x])
        low = jnp.zeros((8, lz), F32)
        high = jnp.zeros((8, lz), F32)
        for k in range(1, 5):
            low = low + taps[k - 1] * jnp.where(sub8 < k, pltpu.roll(h, k, 0), 0.0)
            high = high + taps[k - 1] * jnp.where(sub8 >= 8 - k, pltpu.roll(h, 8 - k, 0), 0.0)
        parts = [acc[:8] + low] + ([acc[8:-8]] if ly > 16 else []) + [acc[-8:] + high]
        return jnp.concatenate(parts, axis=0)

    def publish(par, x, m, packed):
        mp[par, 4 + x, pl.ds(8, ly)] = m
        yp[par, x] = jnp.where(sub8 < 4, m[:8], m[-8:])
        turned = pltpu.roll(m, (8 * x + 4) % lz, 1)
        return jnp.where((lane >= 8 * x) & (lane < 8 * x + 8), turned, packed)

    def fold(v):
        v = jnp.sum(v, axis=0, keepdims=True)
        return v + pltpu.roll(v, lz // 2, 1)

    def pair_row(gamma, delta):
        return jnp.where(row_lane < lz // 2, fold(gamma), fold(delta))

    def unpair(row):
        gamma = jnp.sum(jnp.where(row_lane < lz // 2, row, 0.0), axis=1, keepdims=True)
        delta = jnp.sum(jnp.where(row_lane < lz // 2, 0.0, row), axis=1, keepdims=True)
        return jnp.broadcast_to(gamma, (1, lz)), jnp.broadcast_to(delta, (1, lz))

    hidden = dot(w1[...], feats[...])
    hidden = (hidden * sigmoid(hidden)).astype(BF16)
    hidden = dot(w2[...], hidden)
    hidden = (hidden * sigmoid(hidden)).astype(BF16)
    predicted = dot(w3[...], hidden)
    trace = (predicted[0:1] + predicted[1:2] + predicted[2:3]) / 3.0
    ex, ey, ez = lx // EL, ly // EL, lz // EL
    spread = jnp.where(
        lax.broadcasted_iota(jnp.int32, (lz, lz), 0) == lax.broadcasted_iota(jnp.int32, (lz, lz), 1) // EL,
        1.0,
        0.0,
    )
    lines = jnp.concatenate(
        [trace if e == 0 else pltpu.roll(trace, (lz - e * ez) % lz, 1) for e in range(ex * ey)], axis=0
    )
    forcing = dot(lines, spread, precision=lax.Precision.HIGHEST)
    packed = jnp.zeros((ly, lz), F32)
    for x in range(lx):
        line = forcing[(x // EL) * ey : (x // EL) * ey + ey]
        block = jnp.concatenate([jnp.broadcast_to(line[j : j + 1], (EL, lz)) for j in range(ey)], axis=0)
        source = right[x] + block
        scale = 1.0 / (diag[x] + center)
        inv[x] = scale
        resid[x] = source
        packed = publish(1, x, source * scale, packed)
    zp[1] = packed
    press[...] = jnp.zeros_like(press)
    zv[...] = jnp.zeros_like(zv)
    sv[...] = jnp.zeros_like(sv)
    pv[...] = jnp.zeros_like(pv)
    halo_start(1)
    stencil_local(1)
    halo_wait(1)
    zc = z_correction(1)
    packed = jnp.zeros((ly, lz), F32)
    gamma = jnp.zeros((ly, lz), F32)
    delta = jnp.zeros((ly, lz), F32)
    for x in range(lx):
        r = resid[x]
        scale = inv[x]
        u = r * scale
        w = r - corrected(1, x, zc)
        wv[x] = w
        gamma = gamma + r * u
        delta = delta + w * u
        packed = publish(0, x, w * scale, packed)
    zp[0] = packed
    halo_sent(1)

    def coefficients(first, gamma, delta, gamma_old, alpha_old):
        beta = jnp.where(first, 0.0, gamma / gamma_old)
        return beta, gamma / (delta - beta * gamma / alpha_old)

    def iteration(i, carry):
        gamma_old, alpha_old, row = carry
        par = lax.rem(i, 2)
        later = 1 - par
        sum_start(par, 0, row)
        halo_start(par)
        stencil_local(par)
        for phase in range(1, len(PHASES)):
            sum_start(par, phase, sum_wait(par, phase - 1))
        halo_wait(par)
        zc = z_correction(par)
        for x in range(lx):
            nb[x] = corrected(par, x, zc)
        gamma, delta = unpair(sum_wait(par, len(PHASES) - 1))
        beta, alpha = coefficients(i == 0, gamma, delta, gamma_old, alpha_old)
        packed = jnp.zeros((ly, lz), F32)
        gamma_sum = jnp.zeros((ly, lz), F32)
        delta_sum = jnp.zeros((ly, lz), F32)
        for x in range(lx):
            r, w, scale = resid[x], wv[x], inv[x]
            z = (w - nb[x]) + beta * zv[x]
            s = w + beta * sv[x]
            p = r * scale + beta * pv[x]
            zv[x] = z
            sv[x] = s
            pv[x] = p
            press[x] = press[x] + alpha * p
            r = r - alpha * s
            w = w - alpha * z
            resid[x] = r
            wv[x] = w
            u = r * scale
            gamma_sum = gamma_sum + r * u
            delta_sum = delta_sum + w * u
            packed = publish(later, x, w * scale, packed)
        zp[later] = packed
        halo_sent(par)
        sums_sent(par)
        return gamma, alpha, pair_row(gamma_sum, delta_sum)

    ones = jnp.ones((1, lz), F32)
    gamma_old, alpha_old, row = lax.fori_loop(
        0, ITERS - 1, iteration, (ones, ones, pair_row(gamma, delta))
    )
    par = (ITERS - 1) % 2
    sum_start(par, 0, row)
    for phase in range(1, len(PHASES)):
        sum_start(par, phase, sum_wait(par, phase - 1))
    gamma, delta = unpair(sum_wait(par, len(PHASES) - 1))
    beta, alpha = coefficients(ITERS == 1, gamma, delta, gamma_old, alpha_old)
    for x in range(lx):
        r = resid[x]
        s = wv[x] + beta * sv[x]
        p = r * inv[x] + beta * pv[x]
        press[x] = press[x] + alpha * p
        resid[x] = r - alpha * s
    sums_sent(par)


def pressure_solve(right_side, diagonal, feats, w1, w2, w3):
    sizes = {a: lax.axis_size(a) for a in AXES}
    lx, ly, lz = right_side.shape
    slots = 0
    for axes in PHASES:
        n = 1
        for a in axes:
            n *= sizes[a]
        slots += n
    field = pltpu.VMEM((lx, ly, lz), F32)
    vmem = pl.BlockSpec(memory_space=pltpu.VMEM)
    return pl.pallas_call(
        functools.partial(solve_kernel, sizes),
        out_shape=[jax.ShapeDtypeStruct((lx, ly, lz), F32)] * 2,
        in_specs=[vmem] * 6,
        out_specs=[vmem] * 2,
        scratch_shapes=[
            pltpu.VMEM((2, lx + 8, ly + 16, lz), F32),
            field, field, field, field, field, field,
            pltpu.VMEM((2, lx, 8, lz), F32),
            pltpu.VMEM((2, 2, lx, 8, lz), F32),
            pltpu.VMEM((2, ly, lz), F32),
            pltpu.VMEM((2, 2, ly, lz), F32),
            pltpu.VMEM((2, len(PHASES), 1, lz), F32),
            pltpu.VMEM((2, slots, 1, lz), F32),
            pltpu.SemaphoreType.DMA((6,)),
            pltpu.SemaphoreType.DMA((2, 6)),
            pltpu.SemaphoreType.DMA((slots,)),
            pltpu.SemaphoreType.DMA((2, slots)),
        ],
        compiler_params=pltpu.CompilerParams(collective_id=0, has_side_effects=True),
        cost_estimate=pl.CostEstimate(
            flops=60_000_000, bytes_accessed=200_000_000, transcendentals=0
        ),
    )(right_side, diagonal, feats, w1, w2, w3)


def normalize(gradient):
    return gradient * lax.rsqrt(jnp.mean(gradient * gradient) + epsilon)


def body(
    right_side, diagonal, element_features, sample_bank, target_bank, patch_index, w_first, w_second, w_third
):
    grads = closure_gradients(sample_bank, target_bank, patch_index, w_first, w_second, w_third)
    grads = lax.psum(tuple(grads), AXES)
    pressure, residual = pressure_solve(
        right_side, diagonal, element_features, w_first, w_second, w_third
    )
    steps = tuple(normalize(g) for g in grads)
    return (pressure, residual) + steps


def solution(mesh):
    return jax.shard_map(
        body,
        mesh=mesh,
        in_specs=(
            P("gx", "ga", "gz"),
            P("gx", "ga", "gz"),
            P(None, ("gx", "gz", "ga")),
            P(None, ("gx", "gz", "ga")),
            P(None, ("gx", "gz", "ga")),
            P(("gx", "gz", "ga")),
            P(),
            P(),
            P(),
        ),
        out_specs=(P("gx", "ga", "gz"), P("gx", "ga", "gz"), P(), P(), P()),
        check_vma=False,
    )
```

time: 1050 us -> 175 us (0.17); the launches traced: 1040 us -> 174 us
  blocking collectives: 554 us -> 42.2 us
  starting transfers between devices: 167 us -> 0.04 us
  waiting for transfers between devices: 150 us -> 0.02 us
  Pallas kernels: 0 us -> 107 us
  between operations: 63.5 us -> 16.1 us
  other arithmetic: 49.2 us -> 6.25 us
  local copies, waits for them, and re-layouts: 34.4 us -> 2.38 us
  matrix products: 17.4 us -> 0 us
    psum x12 -> x1, blocking collectives: 554 us -> 42.2 us  [body(): grads = lax.psum(tuple(grads), AXES)]
    ppermute x72 -> x0, starting transfers between devices: 167 us -> none  [the longest x36 121 us: with_halo(): before = lax.ppermute(last, axis, up)]
    pallas_call x0 -> x2, Pallas kernels: none -> 107 us  [the longest x1 93.9 us: pressure_solve(): pl.pallas_call(functools.partial(solve_kernel, sizes), out_shape=[jax.Sha...]
    ppermute x72 -> x0, waiting for transfers between devices: 96.9 us -> none  [the longest x36 76.2 us: with_halo(): after = lax.ppermute(initial, axis, down)]
    psum x1, waiting for transfers between devices: 53.6 us -> 0.01 us  [body(): grads = lax.psum(tuple(grads), AXES)]
    gather x3 -> x0, local copies, waits for them, and re-layouts: 19.9 us -> none  [the longest x2 10.9 us: body(): targets = jnp.take(target_bank, patch_index, axis=1)]
    reduce_sum x12 -> x0, other arithmetic: 18.9 us -> none  [paired_sums(): jnp.sum(scaled * image_dir)]
    dot_general x9 -> x0, matrix products: 17.4 us -> none  [the longest x1 4.07 us: gradients(): lax.dot_general(delta_first, inputs, contract, preferred_element_type=jnp...]
  transfers between devices with their start and end apart: 73 -> 1, of which waited for: 47 -> 0; matrix products, arithmetic and copies ran while one was open for 5% -> 1% of each run, Pallas kernels for 0% -> 54%
where the time goes in v1:
time: 175 us; the launch traced here: 174 us
  Pallas kernels  107 us (61%)
  blocking collectives  42.2 us (24%)
  between operations  16.1 us (9%)
  other arithmetic  6.25 us (4%)
  local copies, waits for them, and re-layouts  2.38 us (1%)
    pallas_call x1, Pallas kernels, pressure_solve(): pl.pallas_call(functools.partial(solve_kernel, sizes), out_shape=[jax.Sha...  93.9 us
    psum x1, blocking collectives, body(): grads = lax.psum(tuple(grads), AXES)  42.2 us
    pallas_call x1, Pallas kernels, closure_gradients(): pl.pallas_call(grad_kernel, grid=(columns // TILE,), in_specs=[pl.BlockSp...  13.5 us
    mul x3, other arithmetic, normalize(): return gradient * lax.rsqrt(jnp.mean(gradient * gradient) + epsilon)  3.95 us
  transfers between devices with their start and end apart: 1, of which 0 were waited for; matrix products, arithmetic and copies ran while one was open for 1% of the time, Pallas kernels for 54%

profile of v1, /device:TPU:0, one launch (start us, length us, event | category | flops | bytes accessed | tf_op | source)
XLA Modules:
  0.0 174.4 jit_solution(17218463461379783776)
XLA Ops:
  7.2 0.0 all-reduce.3.cloned.1.call-start
  7.2 13.5 %shard_map.129 = (f32[256,256]{1,0:T(8,128)}, f32[256,256]{1,0:T(8,128)}, f32[6,256]{1,0:T(8,128)}) custom-call(bf16[256,4096]{1,0:T(8,128)(2,1)} %bank.1, bf16[6,4096]{1,0:T(8,128)(2,1)} %target.1, s32[1,2048]{1,0:T(1,128)} %bitcast.1, bf16[256,256]{1,0:T(8,128)(2,1)} %w1.3, bf16[256,256]{1,0:T(8,128)(2,1)} %w2.3, bf16[6,256]{1,0:T(8,128)(2,1)} %w3.3), custom_call_target="tpu_custom_call" | custom-call | flops 3758096384 | bytes 2097152 | tf_op jit(solution)/shard_map/pallas_call | solution.py:81
  20.7 0.0 all-reduce.3.cloned.1.call-update
  20.7 42.2 %psum.23 = f32[6,256]{1,0:T(8,128)S(1)} all-reduce(f32[6,256]{1,0:T(8,128)} %get-tuple-element.14), channel_id=1, replica_groups=mesh['gx'=2,'gz'=4,'ga'=4] {'gx','gz','ga'}, use_global_device_ids=true, to_apply=%region_4.0 | all-reduce | flops 1536 | bytes 12288 | tf_op jit(solution)/shard_map/psum | solution.py:470
  62.9 0.6 multiply_reduce_fusion.2
  64.2 93.9 %shard_map.128 = (f32[16,32,128]{2,1,0:T(8,128)}, f32[16,32,128]{2,1,0:T(8,128)}) custom-call(f32[16,32,128]{2,1,0:T(8,128)} %right.1, f32[16,32,128]{2,1,0:T(8,128)} %diag.1, bf16[256,128]{1,0:T(8,128)(2,1)} %feats.1, bf16[256,256]{1,0:T(8,128)(2,1)} %w1.3, bf16[256,256]{1,0:T(8,128)(2,1)} %w2.3, bf16[6,256]{1,0:T(8,128)(2,1)} %w3.3), custom_call_target="tpu_custom_call" | custom-call | flops 60000000 | bytes 200000000 | tf_op jit(solution)/shard_map/pallas_call | solution.py:436
  158.1 0.0 copy-start
  158.1 0.6 broadcast_multiply_fusion.2
  158.7 0.0 all-reduce.3.cloned.1.call-done
  158.7 1.7 multiply_reduce_fusion
  161.1 1.7 broadcast_multiply_fusion
  163.5 1.7 broadcast_multiply_fusion.1
  165.1 1.7 copy.18
  166.8 0.0 copy-done
  166.8 0.7 copy.19
Async XLA Ops:
  7.2 151.5 %all-reduce.3.cloned.1.call-start = ((), (), s32[]{:S(2)}) async-start(), calls=%async_computation | async-start | bytes 1048576 | tf_op jit(solution)/shard_map/psum | solution.py:470
  158.1 8.7 %copy-start = (f32[16,32,128]{2,1,0:T(8,128)S(1)}, f32[16,32,128]{2,1,0:T(8,128)}, u32[]{:S(2)}) copy-start(f32[16,32,128]{2,1,0:T(8,128)} %get-tuple-element.25) | copy-start | bytes 786436
Sparse Core Ops, SparseCore 0:
  20.8 132.4 all-reduce.2

commit v2 on v1

--- a/solution.py
+++ b/solution.py
@@ -29,7 +29,7 @@
     return 1.0 / (1.0 + jnp.exp(-v))
 
 
-def grad_kernel(bank, target, index, w1, w2, w3, g1, g2, g3, counts):
+def grad_kernel(bank, target, index, w1, w2, w3, grads, counts):
     step = pl.program_id(0)
     rows = TILE // 128
 
@@ -45,12 +45,12 @@
             jnp.where(low, 1.0, 0.0).astype(BF16),
             ((1,), (1,)),
         )
-        g1[...] = jnp.zeros_like(g1)
-        g2[...] = jnp.zeros_like(g2)
-        g3[...] = jnp.zeros_like(g3)
+        grads[...] = jnp.zeros_like(grads)
 
     weight = jnp.concatenate([counts[pl.ds(step * rows + j, 1), :] for j in range(rows)], axis=1)
     x = bank[...]
+    ch = x.shape[0]
+    stress = target.shape[0]
     a1, a2, a3 = w1[...], w2[...], w3[...]
     l1 = dot(a1, x)
     s1 = sigmoid(l1)
@@ -66,14 +66,14 @@
         lower = (scaled - upper.astype(F32)).astype(BF16)
         return dot(upper, right, ((1,), (1,))) + dot(lower, right, ((1,), (1,)))
 
-    g3[...] += weighted(error, h2)
+    grads[2 * ch : 2 * ch + stress] += weighted(error, h2)
     d2 = (dot(a3, error, ((0,), (0,))) * (s2 * (1.0 + l2 * (1.0 - s2)))).astype(BF16)
-    g2[...] += weighted(d2, h1)
+    grads[ch : 2 * ch] += weighted(d2, h1)
     d1 = (dot(a2, d2, ((0,), (0,))) * (s1 * (1.0 + l1 * (1.0 - s1)))).astype(BF16)
-    g1[...] += weighted(d1, x)
-
-
-def closure_gradients(bank, target, index, w1, w2, w3):
+    grads[:ch] += weighted(d1, x)
+
+
+def closure_gradients(bank, target, index, w1, w2, w3, rows):
     ch, columns = bank.shape
     stress = target.shape[0]
     whole = pl.BlockSpec(memory_space=pltpu.VMEM)
@@ -89,12 +89,8 @@
             whole,
             whole,
         ],
-        out_specs=[fixed((ch, ch)), fixed((ch, ch)), fixed((stress, ch))],
-        out_shape=[
-            jax.ShapeDtypeStruct((ch, ch), F32),
-            jax.ShapeDtypeStruct((ch, ch), F32),
-            jax.ShapeDtypeStruct((stress, ch), F32),
-        ],
+        out_specs=fixed((rows, ch)),
+        out_shape=jax.ShapeDtypeStruct((rows, ch), F32),
         scratch_shapes=[pltpu.VMEM((columns // 128, 128), F32)],
         compiler_params=pltpu.CompilerParams(dimension_semantics=("arbitrary",)),
         cost_estimate=pl.CostEstimate(
@@ -111,8 +107,9 @@
 
 
 def solve_kernel(
-    sizes, right, diag, feats, w1, w2, w3, press, resid,
+    sizes, right, diag, feats, w1, w2, w3, grads, press, resid, step1, step2, step3,
     mp, nb, wv, zv, sv, pv, inv, yp, yr, zp, zr, ar_src, ar_dst,
+    first, held, second, owned, third, full, g_send, g_recv,
     h_send, h_recv, a_send, a_recv,
 ):
     lx, ly, lz = right.shape
@@ -141,6 +138,125 @@
             source = flat(axes, coords(axes, offs, -1))
             peers.append((to, source))
         groups.append((me, peers))
+
+    nx, nz, na = sizes["gx"], sizes["gz"], sizes["ga"]
+    share = grads.shape[0] // nz
+    piece = share // na
+
+    def block_of(iz, ia=None):
+        if ia is None:
+            return pl.ds(pl.multiple_of(iz * share, 8), share)
+        return pl.ds(pl.multiple_of((iz * na + ia) * piece, 8), piece)
+
+    def along(axis, k, sign):
+        return coords((axis,), (k,), sign)[axis]
+
+    def gather_copy(number, axis, k, src, dst):
+        return pltpu.make_async_remote_copy(
+            src_ref=src,
+            dst_ref=dst,
+            send_sem=g_send.at[number],
+            recv_sem=g_recv.at[number],
+            device_id={**pos, axis: along(axis, k, 1)},
+            device_id_type=MESH,
+        )
+
+    def scatter_gz(k):
+        return gather_copy(k - 1, "gz", k, grads.at[block_of(along("gz", k, 1))], first.at[k - 1])
+
+    def scatter_ga(k):
+        rows = pl.ds(pl.multiple_of(along("ga", k, 1) * piece, 8), piece)
+        return gather_copy(nz - 1 + k - 1, "ga", k, held.at[rows], second.at[k - 1])
+
+    def add_gx(k, sign=1):
+        slot = pos["gx"] if sign > 0 else along("gx", k, -1)
+        return gather_copy(nz + na - 2 + k - 1, "gx", k, owned, third.at[slot])
+
+    def gather_ga(k, sign=1):
+        at = pos["ga"] if sign > 0 else along("ga", k, -1)
+        rows = block_of(pos["gz"], at)
+        return gather_copy(nz + na + nx - 3 + k - 1, "ga", k, full.at[rows], full.at[rows])
+
+    def gather_gz(k, sign=1):
+        at = pos["gz"] if sign > 0 else along("gz", k, -1)
+        rows = block_of(at)
+        return gather_copy(nz + 2 * na + nx - 4 + k - 1, "gz", k, full.at[rows], full.at[rows])
+
+    def gradient_prepare(i):
+        @pl.when(i == 3)
+        def _():
+            total = grads[block_of(pos["gz"]), :]
+            for k in range(1, nz):
+                scatter_gz(k).wait_recv()
+                total = total + first[k - 1]
+            held[...] = total
+
+        @pl.when(i == 4)
+        def _():
+            total = held[pl.ds(pl.multiple_of(pos["ga"] * piece, 8), piece), :]
+            for k in range(1, na):
+                scatter_ga(k).wait_recv()
+                total = total + second[k - 1]
+            owned[...] = total
+            third[pos["gx"]] = total
+
+        @pl.when(i == 5)
+        def _():
+            for k in range(1, nx):
+                add_gx(k, -1).wait_recv()
+            full[block_of(pos["gz"], pos["ga"]), :] = jnp.sum(third[...], axis=0)
+
+        @pl.when(i == 6)
+        def _():
+            for k in range(1, na):
+                gather_ga(k, -1).wait_recv()
+
+    def gradient_send(i):
+        for turn in range(3):
+
+            @pl.when(i == turn)
+            def _():
+                for k in range(1 + turn, nz, 3):
+                    scatter_gz(k).start()
+
+            @pl.when(i == 6 + turn)
+            def _():
+                for k in range(1 + turn, nz, 3):
+                    gather_gz(k).start()
+
+        @pl.when(i == 3)
+        def _():
+            for k in range(1, na):
+                scatter_ga(k).start()
+
+        @pl.when(i == 4)
+        def _():
+            for k in range(1, nx):
+                add_gx(k).start()
+
+        @pl.when(i == 5)
+        def _():
+            for k in range(1, na):
+                gather_ga(k).start()
+
+    def gradient_finish():
+        for k in range(1, nz):
+            gather_gz(k, -1).wait_recv()
+            scatter_gz(k).wait_send()
+            gather_gz(k).wait_send()
+        for k in range(1, na):
+            scatter_ga(k).wait_send()
+            gather_ga(k).wait_send()
+        for k in range(1, nx):
+            add_gx(k).wait_send()
+        ch = step1.shape[0]
+        start = 0
+        for out in (step1, step2, step3):
+            count = out.shape[0]
+            value = full[start : start + count]
+            squares = jnp.sum(jnp.sum(value * value, axis=0, keepdims=True), axis=1, keepdims=True)
+            out[...] = value * lax.rsqrt(squares / (count * ch) + epsilon)
+            start += count
 
     mp[...] = jnp.zeros_like(mp)
     yr[...] = jnp.zeros_like(yr)
@@ -370,8 +486,10 @@
         sum_start(par, 0, row)
         halo_start(par)
         stencil_local(par)
+        gradient_prepare(i)
         for phase in range(1, len(PHASES)):
             sum_start(par, phase, sum_wait(par, phase - 1))
+        gradient_send(i)
         halo_wait(par)
         zc = z_correction(par)
         for x in range(lx):
@@ -409,6 +527,7 @@
     )
     par = (ITERS - 1) % 2
     sum_start(par, 0, row)
+    gradient_finish()
     for phase in range(1, len(PHASES)):
         sum_start(par, phase, sum_wait(par, phase - 1))
     gamma, delta = unpair(sum_wait(par, len(PHASES) - 1))
@@ -422,7 +541,7 @@
     sums_sent(par)
 
 
-def pressure_solve(right_side, diagonal, feats, w1, w2, w3):
+def pressure_solve(right_side, diagonal, feats, w1, w2, w3, grads):
     sizes = {a: lax.axis_size(a) for a in AXES}
     lx, ly, lz = right_side.shape
     slots = 0
@@ -431,13 +550,19 @@
         for a in axes:
             n *= sizes[a]
         slots += n
+    nx, nz, na = (sizes[a] for a in ("gx", "gz", "ga"))
+    rows, ch = grads.shape
+    share = rows // nz
+    piece = share // na
+    copies = max(2 * (nz - 1) + 2 * (na - 1) + nx - 1, 1)
     field = pltpu.VMEM((lx, ly, lz), F32)
     vmem = pl.BlockSpec(memory_space=pltpu.VMEM)
     return pl.pallas_call(
         functools.partial(solve_kernel, sizes),
-        out_shape=[jax.ShapeDtypeStruct((lx, ly, lz), F32)] * 2,
-        in_specs=[vmem] * 6,
-        out_specs=[vmem] * 2,
+        out_shape=[jax.ShapeDtypeStruct((lx, ly, lz), F32)] * 2
+        + [jax.ShapeDtypeStruct(w.shape, F32) for w in (w1, w2, w3)],
+        in_specs=[vmem] * 7,
+        out_specs=[vmem] * 5,
         scratch_shapes=[
             pltpu.VMEM((2, lx + 8, ly + 16, lz), F32),
             field, field, field, field, field, field,
@@ -447,6 +572,14 @@
             pltpu.VMEM((2, 2, ly, lz), F32),
             pltpu.VMEM((2, len(PHASES), 1, lz), F32),
             pltpu.VMEM((2, slots, 1, lz), F32),
+            pltpu.VMEM((max(nz - 1, 1), share, ch), F32),
+            pltpu.VMEM((share, ch), F32),
+            pltpu.VMEM((max(na - 1, 1), piece, ch), F32),
+            pltpu.VMEM((piece, ch), F32),
+            pltpu.VMEM((nx, piece, ch), F32),
+            pltpu.VMEM((rows, ch), F32),
+            pltpu.SemaphoreType.DMA((copies,)),
+            pltpu.SemaphoreType.DMA((copies,)),
             pltpu.SemaphoreType.DMA((6,)),
             pltpu.SemaphoreType.DMA((2, 6)),
             pltpu.SemaphoreType.DMA((slots,)),
@@ -456,23 +589,23 @@
         cost_estimate=pl.CostEstimate(
             flops=60_000_000, bytes_accessed=200_000_000, transcendentals=0
         ),
-    )(right_side, diagonal, feats, w1, w2, w3)
-
-
-def normalize(gradient):
-    return gradient * lax.rsqrt(jnp.mean(gradient * gradient) + epsilon)
+    )(right_side, diagonal, feats, w1, w2, w3, grads)
 
 
 def body(
     right_side, diagonal, element_features, sample_bank, target_bank, patch_index, w_first, w_second, w_third
 ):
-    grads = closure_gradients(sample_bank, target_bank, patch_index, w_first, w_second, w_third)
-    grads = lax.psum(tuple(grads), AXES)
-    pressure, residual = pressure_solve(
-        right_side, diagonal, element_features, w_first, w_second, w_third
+    unit = 8 * lax.axis_size("gz") * lax.axis_size("ga")
+    rows = w_first.shape[0] + w_second.shape[0] + w_third.shape[0]
+    rows = (rows + unit - 1) // unit * unit
+    grads = closure_gradients(
+        sample_bank, target_bank, patch_index, w_first, w_second, w_third, rows
     )
-    steps = tuple(normalize(g) for g in grads)
-    return (pressure, residual) + steps
+    return tuple(
+        pressure_solve(
+            right_side, diagonal, element_features, w_first, w_second, w_third, grads
+        )
+    )
 
 
 def solution(mesh):

time: 175 us -> 118 us (0.67)
  blocking collectives: 42.2 us -> 0 us
  between operations: 16.1 us -> 0.65 us
  other arithmetic: 6.25 us -> 0 us
  local copies, waits for them, and re-layouts: 2.38 us -> 7.29 us
  Pallas kernels: 107 us -> 110 us
    psum x1 -> x0, blocking collectives: 42.2 us -> none  [body(): grads = lax.psum(tuple(grads), AXES)]
    unnamed x4 -> x7, local copies, waits for them, and re-layouts: 2.38 us -> 7.29 us
    mul x3 -> x0, other arithmetic: 3.95 us -> none  [normalize(): return gradient * lax.rsqrt(jnp.mean(gradient * gradient) + epsilon)]
    pallas_call x1, Pallas kernels: 93.9 us -> 96.7 us  [pressure_solve(): pl.pallas_call(functools.partial(solve_kernel, sizes), out_shape=[jax.Sha...]
    reduce_sum x2 -> x0, other arithmetic: 2.3 us -> none  [normalize(): return gradient * lax.rsqrt(jnp.mean(gradient * gradient) + epsilon)]
  transfers between devices with their start and end apart: 1 -> 0, of which waited for: 0 -> 0; matrix products, arithmetic and copies ran while one was open for 1% -> 0% of each run, Pallas kernels for 54% -> 0%
where the time goes in v2:
time: 118 us
  Pallas kernels  110 us (93%)
  local copies, waits for them, and re-layouts  7.29 us (6%)
    pallas_call x1, Pallas kernels, pressure_solve(): pl.pallas_call(functools.partial(solve_kernel, sizes), out_shape=[jax.Sha...  96.7 us
    pallas_call x1, Pallas kernels, closure_gradients(): pl.pallas_call(grad_kernel, grid=(columns // TILE,), in_specs=[pl.BlockSp...  13.6 us
    unnamed x7, local copies, waits for them, and re-layouts  7.29 us

profile of v2, /device:TPU:0, one launch (start us, length us, event | category | flops | bytes accessed | tf_op | source)
XLA Modules:
  0.0 118.1 jit_solution(1916504011279470385)
XLA Ops:
  0.6 13.6 %shard_map.128.grads = f32[640,256]{1,0:T(8,128)} custom-call(bf16[256,4096]{1,0:T(8,128)(2,1)} %bank.1, bf16[6,4096]{1,0:T(8,128)(2,1)} %target.1, s32[1,2048]{1,0:T(1,128)} %bitcast.1, bf16[256,256]{1,0:T(8,128)(2,1)} %w1.3, bf16[256,256]{1,0:T(8,128)(2,1)} %w2.3, bf16[6,256]{1,0:T(8,128)(2,1)} %w3.3), custom_call_target="tpu_custom_call" | custom-call | flops 3758096384 | bytes 2097152 | tf_op jit(solution)/shard_map/pallas_call | solution.py:81
  14.2 96.7 %shard_map.129 = (f32[16,32,128]{2,1,0:T(8,128)}, f32[16,32,128]{2,1,0:T(8,128)}, f32[256,256]{1,0:T(8,128)}, f32[256,256]{1,0:T(8,128)}, f32[6,256]{1,0:T(8,128)}) custom-call(f32[16,32,128]{2,1,0:T(8,128)} %right.1, f32[16,32,128]{2,1,0:T(8,128)} %diag.1, bf16[256,128]{1,0:T(8,128)(2,1)} %feats.1, bf16[256,256]{1,0:T(8,128)(2,1)} %w1.3, ...), custom_call_target="tpu_custom_call" | custom-call | flops 60000000 | bytes 200000000 | tf_op jit(solution)/shard_map/pallas_call | solution.py:560
  110.8 0.0 copy-start
  110.9 1.7 %copy.19 = f32[16,32,128]{2,1,0:T(8,128)} copy(f32[16,32,128]{2,1,0:T(8,128)} %get-tuple-element.10) | data formatting | bytes 524288
  112.5 1.7 %copy.20 = f32[16,32,128]{2,1,0:T(8,128)} copy(f32[16,32,128]{2,1,0:T(8,128)} %get-tuple-element.11) | data formatting | bytes 524288
  114.2 1.7 %copy.21 = f32[256,256]{1,0:T(8,128)} copy(f32[256,256]{1,0:T(8,128)} %get-tuple-element.12) | data formatting | bytes 524288
  115.9 1.7 %copy.22 = f32[256,256]{1,0:T(8,128)} copy(f32[256,256]{1,0:T(8,128)} %get-tuple-element.13) | data formatting | bytes 524288
  117.5 0.0 copy-done
  117.5 0.6 copy.23
Async XLA Ops:
  110.8 6.7 %copy-start = (f32[6,256]{1,0:T(8,128)S(1)}, f32[6,256]{1,0:T(8,128)}, u32[]{:S(2)}) copy-start(f32[6,256]{1,0:T(8,128)} %get-tuple-element.14) | copy-start | bytes 18436
